TPU v7x, 256 devices: a whole 4x4x8 slice. The times are simulated.
256 devices in a mesh: scen: 16 (over z, y_hi), gen: 16 (over y_lo, x, core).
Axes of the slice: x: 4, y: 4 (y_hi: 2, y_lo: 2; y = y_hi * 2 + y_lo), z: 8, core: 2. Of those that a mesh axis runs over, the one named last changes fastest.
Arguments:
- zone_load: float32 [256, 16, 256], P('scen'), may hold values from 0.3 to 1
- linear_cost: float32 [16, 20480], P(None, 'gen'), may hold values from -4 to 4
- cost_diag: float32 [20480], P('gen'), may hold values from 0.5 to 2
- capacity: float32 [20480], P('gen'), may hold values from 0.5 to 2
- cost_tiles: bfloat16 [80, 256, 256], P('gen'), may hold values from -0.375 to 0.375
- coupling_tiles: bfloat16 [16, 80, 256, 256], P('scen', 'gen'), may hold values from -0.375 to 0.375
- block_map: int32 [16, 80], P('scen', 'gen'), may hold values 0 or 1
- zone_index: int32 [20480], P('gen'), may hold values from 0 to 255
- step_numer: int32 [5], replicated, may hold values from 1 to 4
- step_denom: int32 [5], replicated, may hold values from 5 to 8
Outputs:
- dispatch: float32 [256, 16, 20480], P('scen', None, 'gen')
- prices: float32 [256, 16, 256], P('scen')
- plan: float32 [16, 20480], P(None, 'gen')
All inputs are finite; a program needn't handle non-finite values. No bound on the sum of `block_map` on one device may be relied on, other than what follows from the above.
Results may differ from a plain program's by a relative error of at most 0.0003.
Values sent between devices are 32-bit elements; how exact they have to be, the bound alone decides.
A program may use at most 64 MiB of HBM per device.

v0:
```python
import jax
import jax.numpy as jnp
from jax import lax
from jax.sharding import Mesh
from jax.sharding import PartitionSpec as P

G = 20480
ITERS = 5
GEN = ("gen_0", "gen_1", "gen_2")
SCEN = ("scen_0", "scen_1")
SCEN_GEN = ("scen_0", "scen_1", "gen_0", "gen_1", "gen_2")
penalty = 2.0
centering = 0.5
epsilon = 1e-06


def copy_for_each(value, axis):
    copies = jnp.broadcast_to(value, (lax.axis_size(axis), *value.shape))
    return lax.all_to_all(copies, axis, split_axis=0, concat_axis=0, tiled=True)


def taken_together(value, axis):
    return copy_for_each(value, axis).sum(axis=0)


def over_pieces(value, axis):
    blocks = lax.all_gather(value, axis)
    return blocks.sum(axis=0)


def by_axis(value, axes):
    for axis in axes:
        value = lax.psum(value, axis)
    return value


def local(
    zone_load,
    linear_cost,
    cost_diag,
    capacity,
    cost_tiles,
    coupling_tiles,
    block_map,
    zone_index,
    step_numer,
    step_denom,
):
    local_scen = zone_load.shape[0]
    periods = linear_cost.shape[0]
    zone_count = zone_load.shape[2]
    local_gen = capacity.shape[0]
    local_blocks = cost_tiles.shape[0]
    tile_width = cost_tiles.shape[2]
    gen_devices = lax.axis_size(GEN)
    total_scen = local_scen * lax.axis_size(SCEN)
    row_count = local_scen * periods
    entries = float(total_scen * periods * G)
    coupling = coupling_tiles[0]
    block_mask = block_map[0].astype(jnp.float32)
    onehot = (zone_index[:, None] == jnp.arange(zone_count, dtype=jnp.int32)[None, :]).astype(
        jnp.float32
    )
    scen_ids = lax.axis_index(SCEN) * local_scen + jnp.arange(local_scen, dtype=jnp.int32)
    levels = 0.2 + 0.6 * (scen_ids.astype(jnp.float32) + 0.5) / total_scen
    dispatch = jnp.broadcast_to(levels[:, None, None] * capacity, (local_scen, periods, local_gen))
    low_dual = jnp.ones((local_scen, periods, local_gen), jnp.float32)
    high_dual = jnp.ones((local_scen, periods, local_gen), jnp.float32)
    prices = jnp.zeros((local_scen, periods, zone_count), jnp.float32)
    lowest = 0.02 * capacity
    highest = 0.98 * capacity
    plan = jnp.zeros((periods, local_gen), jnp.float32)
    for iteration in range(ITERS):
        step_size = step_numer[iteration].astype(jnp.float32) / step_denom[iteration].astype(
            jnp.float32
        )
        column_sums = taken_together(jnp.sum(dispatch, axis=0), SCEN)
        plan = column_sums / total_scen
        partial_value = jnp.dot(
            dispatch.reshape(row_count, local_gen),
            onehot,
            precision=lax.Precision.HIGHEST,
            preferred_element_type=jnp.float32,
        )
        totals = over_pieces(partial_value, GEN)
        imbalance = totals.reshape(local_scen, periods, zone_count) * (zone_count / G) - zone_load
        primal_local = jnp.sum(imbalance * imbalance) / gen_devices
        rounded = dispatch.astype(jnp.bfloat16).reshape(row_count, local_blocks, tile_width)
        cross_part = jnp.einsum(
            "rki,kij->rkj", rounded, coupling, preferred_element_type=jnp.float32
        )
        own_part = jnp.einsum(
            "rki,kij->rkj", rounded, cost_tiles, preferred_element_type=jnp.float32
        )
        products = (own_part + cross_part * block_mask[None, :, None]).reshape(
            local_scen, periods, local_gen
        )
        price_terms = jnp.dot(
            prices.reshape(row_count, zone_count),
            onehot.T,
            precision=lax.Precision.HIGHEST,
            preferred_element_type=jnp.float32,
        )
        residual = (
            cost_diag * dispatch
            + products
            + linear_cost
            + penalty * (dispatch - plan)
            + price_terms.reshape(local_scen, periods, local_gen)
            - low_dual
            + high_dual
        )
        gap_local = jnp.sum(dispatch * low_dual + (capacity - dispatch) * high_dual)
        dual_local = jnp.sum(residual * residual)
        stacked = jnp.stack([gap_local, dual_local, primal_local])
        summed = by_axis(stacked, SCEN_GEN)
        gap_sum = summed[0]
        dual_sq = summed[1]
        primal_sq = summed[2]
        target = centering * gap_sum / (2.0 * entries)
        dual_rms = jnp.sqrt(dual_sq / entries + epsilon)
        primal_rms = jnp.sqrt(primal_sq / float(total_scen * periods * zone_count) + epsilon)
        scaling = cost_diag + penalty + low_dual / dispatch + high_dual / (capacity - dispatch)
        updated = jnp.clip(
            dispatch - step_size * residual / (scaling * (1.0 + dual_rms)), lowest, highest
        )
        low_dual = low_dual + step_size * (target / updated - low_dual)
        high_dual = high_dual + step_size * (target / (capacity - updated) - high_dual)
        prices = prices + step_size * imbalance / (1.0 + primal_rms)
        dispatch = updated
    return (dispatch, prices, plan)


def solution(mesh):
    torus = Mesh(
        mesh.devices.reshape(8, 2, 2, 4, 2), ("scen_0", "scen_1", "gen_0", "gen_1", "gen_2")
    )
    placed = (
        P(SCEN, None, None),
        P(None, GEN),
        P(GEN),
        P(GEN),
        P(GEN, None, None),
        P(SCEN, GEN, None, None),
        P(SCEN, GEN),
        P(GEN),
        P(),
        P(),
    )
    return jax.shard_map(
        local,
        mesh=torus,
        in_specs=placed,
        out_specs=(P(SCEN, None, GEN), P(SCEN, None, None), P(None, GEN)),
        check_vma=False,
    )
```

profile of v0, /device:TPU:1, one launch (start us, length us, event | category | flops | bytes accessed | tf_op | source)
XLA Modules:
  0.0 563.8 jit_solution(9734501786071534831)
XLA Ops:
  11.2 11.8 %all-to-all-start = ((f32[16,16,1280]{2,1,0:T(8,128)}), f32[16,16,1280]{2,1,0:T(8,128)}, u32[]{:S(2)}, u32[]{:S(2)}) async-start(f32[16,16,1280]{2,1,0:T(8,128)} %broadcast_in_dim.30), calls=%async_computation | async-start | bytes 2621440 | tf_op jit(solution)/shard_map/all_to_all | solution.py:19
  25.3 2.1 copy.38
  30.3 24.3 %all-to-all-done = f32[16,16,1280]{2,1,0:T(8,128)} async-done(((f32[16,16,1280]{2,1,0:T(8,128)}), f32[16,16,1280]{2,1,0:T(8,128)}, u32[]{:S(2)}, u32[]{:S(2)}) %all-to-all-start) | async-done | bytes 1310752 | tf_op jit(solution)/shard_map/all_to_all | solution.py:19
  56.0 2.7 multiply_reduce_fusion.4
  58.7 6.3 %all-gather.11.cloned.1.call-done = f32[4096,256]{1,0:T(8,128)} async-done(((f32[256,256]{1,0:T(8,128)}), f32[4096,256]{1,0:T(8,128)}) %all-gather.11.cloned.1.call-update) | async-done | bytes 4194320 | tf_op jit(solution)/shard_map/all_gather | solution.py:27
  65.0 2.5 reduce_sum.274
  70.8 14.7 %psum.175 = f32[3]{0:T(128)S(1)} all-reduce(f32[3]{0:T(128)S(1)} %pad_maximum_fusion), channel_id=1, replica_groups=mesh['scen_0'=8,'scen_1'=2,'gen_0'=2,'gen_1'=4,'gen_2'=2] {'scen_0'}, use_global_device_ids=true, to_apply=%region_6.0 | all-reduce | flops 3 | bytes 24 | tf_op jit(solution)/shard_map/psum | solution.py:33
  86.1 5.3 psum.176
  92.0 4.1 psum.177
  96.8 7.0 %psum.178 = f32[3]{0:T(128)S(1)} all-reduce(f32[3]{0:T(128)S(1)} %psum.177), channel_id=1, replica_groups=mesh['scen_0'=8,'scen_1'=2,'gen_0'=2,'gen_1'=4,'gen_2'=2] {'gen_1'}, use_global_device_ids=true, to_apply=%region_9.0 | all-reduce | flops 3 | bytes 24 | tf_op jit(solution)/shard_map/psum | solution.py:33
  103.8 10.2 %psum.179 = f32[3]{0:T(128)S(1)} all-reduce(f32[3]{0:T(128)S(1)} %psum.178), channel_id=1, replica_groups=mesh['scen_0'=8,'scen_1'=2,'gen_0'=2,'gen_1'=4,'gen_2'=2] {'gen_2'}, use_global_device_ids=true, to_apply=%region_10.0 | all-reduce | flops 3 | bytes 24 | tf_op jit(solution)/shard_map/psum | solution.py:33
  115.9 2.9 add_reduce_fusion.3
  121.7 6.3 %all-to-all-start.1 = ((f32[16,16,1280]{2,1,0:T(8,128)}), f32[16,16,1280]{2,1,0:T(8,128)}, u32[]{:S(2)}, u32[]{:S(2)}) async-start(f32[16,16,1280]{2,1,0:T(8,128)} %broadcast_in_dim.32), calls=%async_computation.1 | async-start | bytes 2621440 | tf_op jit(solution)/shard_map/all_to_all | solution.py:19
  132.9 2.1 copy.41
  137.0 22.9 %all-to-all-done.1 = f32[16,16,1280]{2,1,0:T(8,128)} async-done(((f32[16,16,1280]{2,1,0:T(8,128)}), f32[16,16,1280]{2,1,0:T(8,128)}, u32[]{:S(2)}, u32[]{:S(2)}) %all-to-all-start.1) | async-done | bytes 1310752 | tf_op jit(solution)/shard_map/all_to_all | solution.py:19
  162.8 4.6 multiply_reduce_fusion.3
  167.4 2.5 reduce_sum.280
  172.5 14.5 %psum.180 = f32[3]{0:T(128)S(1)} all-reduce(f32[3]{0:T(128)S(1)} %pad_maximum_fusion.1), channel_id=1, replica_groups=mesh['scen_0'=8,'scen_1'=2,'gen_0'=2,'gen_1'=4,'gen_2'=2] {'scen_0'}, use_global_device_ids=true, to_apply=%region_17.18 | all-reduce | flops 3 | bytes 24 | tf_op jit(solution)/shard_map/psum | solution.py:33
  186.9 5.3 psum.181
  192.9 4.1 psum.182
  197.6 6.3 %psum.183 = f32[3]{0:T(128)S(1)} all-reduce(f32[3]{0:T(128)S(1)} %psum.182), channel_id=1, replica_groups=mesh['scen_0'=8,'scen_1'=2,'gen_0'=2,'gen_1'=4,'gen_2'=2] {'gen_1'}, use_global_device_ids=true, to_apply=%region_20.21 | all-reduce | flops 3 | bytes 24 | tf_op jit(solution)/shard_map/psum | solution.py:33
  204.0 10.3 %psum.184 = f32[3]{0:T(128)S(1)} all-reduce(f32[3]{0:T(128)S(1)} %psum.183), channel_id=1, replica_groups=mesh['scen_0'=8,'scen_1'=2,'gen_0'=2,'gen_1'=4,'gen_2'=2] {'gen_2'}, use_global_device_ids=true, to_apply=%region_21.22 | all-reduce | flops 3 | bytes 24 | tf_op jit(solution)/shard_map/psum | solution.py:33
  216.3 3.9 add_reduce_fusion.2
  223.9 6.5 %all-to-all-start.2 = ((f32[16,16,1280]{2,1,0:T(8,128)}), f32[16,16,1280]{2,1,0:T(8,128)}, u32[]{:S(2)}, u32[]{:S(2)}) async-start(f32[16,16,1280]{2,1,0:T(8,128)} %broadcast_in_dim.33), calls=%async_computation.2 | async-start | bytes 2621440 | tf_op jit(solution)/shard_map/all_to_all | solution.py:19
  232.7 2.5 reshape.274
  237.3 2.1 copy.44
  239.5 2.8 reshape.275
  242.2 20.0 %all-to-all-done.2 = f32[16,16,1280]{2,1,0:T(8,128)} async-done(((f32[16,16,1280]{2,1,0:T(8,128)}), f32[16,16,1280]{2,1,0:T(8,128)}, u32[]{:S(2)}, u32[]{:S(2)}) %all-to-all-start.2) | async-done | bytes 1310752 | tf_op jit(solution)/shard_map/all_to_all | solution.py:19
  265.8 2.7 all-gather.15.cloned.1.call-done
  268.5 3.2 reduce_sum.286
  272.6 2.5 divide_add_fusion.3
  275.8 5.3 multiply_reduce_fusion.2
  282.3 14.8 %psum.185 = f32[3]{0:T(128)S(1)} all-reduce(f32[3]{0:T(128)S(1)} %pad_maximum_fusion.2), channel_id=1, replica_groups=mesh['scen_0'=8,'scen_1'=2,'gen_0'=2,'gen_1'=4,'gen_2'=2] {'scen_0'}, use_global_device_ids=true, to_apply=%region_28.29 | all-reduce | flops 3 | bytes 24 | tf_op jit(solution)/shard_map/psum | solution.py:33
  297.1 5.3 psum.186
  303.0 4.0 psum.187
  307.7 6.7 %psum.188 = f32[3]{0:T(128)S(1)} all-reduce(f32[3]{0:T(128)S(1)} %psum.187), channel_id=1, replica_groups=mesh['scen_0'=8,'scen_1'=2,'gen_0'=2,'gen_1'=4,'gen_2'=2] {'gen_1'}, use_global_device_ids=true, to_apply=%region_31.32 | all-reduce | flops 3 | bytes 24 | tf_op jit(solution)/shard_map/psum | solution.py:33
  314.4 10.2 %psum.189 = f32[3]{0:T(128)S(1)} all-reduce(f32[3]{0:T(128)S(1)} %psum.188), channel_id=1, replica_groups=mesh['scen_0'=8,'scen_1'=2,'gen_0'=2,'gen_1'=4,'gen_2'=2] {'gen_2'}, use_global_device_ids=true, to_apply=%region_32.33 | all-reduce | flops 3 | bytes 24 | tf_op jit(solution)/shard_map/psum | solution.py:33
  326.6 5.3 add_reduce_fusion.1
  334.8 6.7 %all-to-all-start.3 = ((f32[16,16,1280]{2,1,0:T(8,128)}), f32[16,16,1280]{2,1,0:T(8,128)}, u32[]{:S(2)}, u32[]{:S(2)}) async-start(f32[16,16,1280]{2,1,0:T(8,128)} %broadcast_in_dim.34), calls=%async_computation.3 | async-start | bytes 2621440 | tf_op jit(solution)/shard_map/all_to_all | solution.py:19
  346.6 2.1 copy.47
  348.7 2.7 reshape.278
  351.5 21.8 %all-to-all-done.3 = f32[16,16,1280]{2,1,0:T(8,128)} async-done(((f32[16,16,1280]{2,1,0:T(8,128)}), f32[16,16,1280]{2,1,0:T(8,128)}, u32[]{:S(2)}, u32[]{:S(2)}) %all-to-all-start.3) | async-done | bytes 1310752 | tf_op jit(solution)/shard_map/all_to_all | solution.py:19
  376.2 4.8 multiply_reduce_fusion.1
  381.0 3.2 reduce_sum.292
  388.4 15.2 %psum.190 = f32[3]{0:T(128)} all-reduce(f32[3]{0:T(128)} %pad_maximum_fusion.3), channel_id=1, replica_groups=mesh['scen_0'=8,'scen_1'=2,'gen_0'=2,'gen_1'=4,'gen_2'=2] {'scen_0'}, use_global_device_ids=true, to_apply=%region_39.40 | all-reduce | flops 3 | bytes 24 | tf_op jit(solution)/shard_map/psum | solution.py:33
  403.5 5.9 %psum.191 = f32[3]{0:T(128)} all-reduce(f32[3]{0:T(128)} %psum.190), channel_id=1, replica_groups=mesh['scen_0'=8,'scen_1'=2,'gen_0'=2,'gen_1'=4,'gen_2'=2] {'scen_1'}, use_global_device_ids=true, to_apply=%region_40.41 | all-reduce | flops 3 | bytes 24 | tf_op jit(solution)/shard_map/psum | solution.py:33
  410.1 4.6 psum.192
  415.3 7.4 %psum.193 = f32[3]{0:T(128)} all-reduce(f32[3]{0:T(128)} %psum.192), channel_id=1, replica_groups=mesh['scen_0'=8,'scen_1'=2,'gen_0'=2,'gen_1'=4,'gen_2'=2] {'gen_1'}, use_global_device_ids=true, to_apply=%region_42.43 | all-reduce | flops 3 | bytes 24 | tf_op jit(solution)/shard_map/psum | solution.py:33
  422.7 11.6 %psum.194 = f32[3]{0:T(128)} all-reduce(f32[3]{0:T(128)} %psum.193), channel_id=1, replica_groups=mesh['scen_0'=8,'scen_1'=2,'gen_0'=2,'gen_1'=4,'gen_2'=2] {'gen_2'}, use_global_device_ids=true, to_apply=%region_43.44 | all-reduce | flops 3 | bytes 24 | tf_op jit(solution)/shard_map/psum | solution.py:33
  437.0 3.8 add_reduce_fusion
  444.7 6.0 %all-to-all-start.4 = ((f32[16,16,1280]{2,1,0:T(8,128)}), f32[16,16,1280]{2,1,0:T(8,128)}, u32[]{:S(2)}, u32[]{:S(2)}) async-start(f32[16,16,1280]{2,1,0:T(8,128)} %broadcast_in_dim.35), calls=%async_computation.4 | async-start | bytes 2621440 | tf_op jit(solution)/shard_map/all_to_all | solution.py:19
  455.5 2.1 copy.50
  457.7 2.8 reshape.281
  460.5 22.0 %all-to-all-done.4 = f32[16,16,1280]{2,1,0:T(8,128)} async-done(((f32[16,16,1280]{2,1,0:T(8,128)}), f32[16,16,1280]{2,1,0:T(8,128)}, u32[]{:S(2)}, u32[]{:S(2)}) %all-to-all-start.4) | async-done | bytes 1310752 | tf_op jit(solution)/shard_map/all_to_all | solution.py:19
  484.5 4.8 all-gather.19.cloned.1.call-done
  489.4 3.2 reduce_sum.298
  493.6 2.6 multiply_reduce_fusion.5
  496.9 5.0 multiply_reduce_fusion
  503.7 15.5 %psum.195 = f32[3]{0:T(128)} all-reduce(f32[3]{0:T(128)} %pad_maximum_fusion.4), channel_id=1, replica_groups=mesh['scen_0'=8,'scen_1'=2,'gen_0'=2,'gen_1'=4,'gen_2'=2] {'scen_0'}, use_global_device_ids=true, to_apply=%region_50.51 | all-reduce | flops 3 | bytes 24 | tf_op jit(solution)/shard_map/psum | solution.py:33
  519.2 5.9 %psum.196 = f32[3]{0:T(128)} all-reduce(f32[3]{0:T(128)} %psum.195), channel_id=1, replica_groups=mesh['scen_0'=8,'scen_1'=2,'gen_0'=2,'gen_1'=4,'gen_2'=2] {'scen_1'}, use_global_device_ids=true, to_apply=%region_51.52 | all-reduce | flops 3 | bytes 24 | tf_op jit(solution)/shard_map/psum | solution.py:33
  525.6 4.4 psum.197
  530.7 7.0 %psum.198 = f32[3]{0:T(128)} all-reduce(f32[3]{0:T(128)} %psum.197), channel_id=1, replica_groups=mesh['scen_0'=8,'scen_1'=2,'gen_0'=2,'gen_1'=4,'gen_2'=2] {'gen_1'}, use_global_device_ids=true, to_apply=%region_53.54 | all-reduce | flops 3 | bytes 24 | tf_op jit(solution)/shard_map/psum | solution.py:33
  537.7 11.1 %psum.199 = f32[3]{0:T(128)} all-reduce(f32[3]{0:T(128)} %psum.198), channel_id=1, replica_groups=mesh['scen_0'=8,'scen_1'=2,'gen_0'=2,'gen_1'=4,'gen_2'=2] {'gen_2'}, use_global_device_ids=true, to_apply=%region_54.55 | all-reduce | flops 3 | bytes 24 | tf_op jit(solution)/shard_map/psum | solution.py:33
  553.3 3.7 maximum_minimum_fusion
  (152 shorter events, 73.8 us)
Async XLA Ops:
  7.2 16.7 %copy-start = (bf16[5,256,256]{2,1,0:T(8,128)(2,1)S(1)}, bf16[5,256,256]{2,1,0:T(8,128)(2,1)}, u32[]{:S(2)}) copy-start(bf16[5,256,256]{2,1,0:T(8,128)(2,1)} %param.14) | copy-start | bytes 1966084
  7.2 1.0 copy-start.21
  7.2 57.8 %all-gather.11.cloned.1.call-start = ((), (), s32[]{:S(2)}) async-start(), calls=%async_computation.5 | async-start | bytes 4456448 | tf_op jit(solution)/shard_map/all_gather | solution.py:27
  8.1 1.8 copy-start.16
  11.2 43.4 %all-to-all-start = ((f32[16,16,1280]{2,1,0:T(8,128)}), f32[16,16,1280]{2,1,0:T(8,128)}, u32[]{:S(2)}, u32[]{:S(2)}) async-start(f32[16,16,1280]{2,1,0:T(8,128)} %broadcast_in_dim.30), calls=%async_computation | async-start | bytes 2621440 | tf_op jit(solution)/shard_map/all_to_all | solution.py:19
  23.0 0.8 copy-start.34
  23.0 144.4 %all-gather.13.cloned.1.call-start = ((), (), s32[]{:S(2)}) async-start(), calls=%async_computation.6 | async-start | bytes 4456448 | tf_op jit(solution)/shard_map/all_gather | solution.py:27
  23.8 1.5 copy-start.27
  23.9 1.1 copy-start.6
  27.5 2.8 copy-start.26
  29.4 26.7 %copy-start.25 = (f32[16,1280]{1,0:T(8,128)S(1)}, f32[16,1280]{1,0:T(8,128)}, u32[]{:S(2)}) copy-start(f32[16,1280]{1,0:T(8,128)} %param.11) | copy-start | bytes 245764
  30.3 85.6 %copy-start.19 = (f32[1280]{0:T(1024)}, f32[1280]{0:T(1024)S(1)}, u32[]{:S(2)}) copy-start(f32[1280]{0:T(1024)S(1)} %get-tuple-element.24) | copy-start | bytes 15364
  30.3 85.6 %copy-start.20 = (f32[1280]{0:T(1024)}, f32[1280]{0:T(1024)S(1)}, u32[]{:S(2)}) copy-start(f32[1280]{0:T(1024)S(1)} %get-tuple-element.25) | copy-start | bytes 15364
  65.0 2.6 copy-start.10
  65.0 5.2 copy-start.32
  65.0 20.5 %copy-start.33 = (s32[5]{0:T(128)S(1)}, s32[5]{0:T(128)}, u32[]{:S(2)}) copy-start(s32[5]{0:T(128)} %param.19) | copy-start | bytes 64
  67.5 48.4 %copy-start.13 = (f32[256,256]{1,0:T(8,128)}, f32[256,256]{1,0:T(8,128)S(1)}, u32[]{:S(2)}) copy-start(f32[256,256]{1,0:T(8,128)S(1)} %reduce_sum.274) | copy-start | bytes 786436
  67.5 48.4 %copy-start.15 = (f32[256,256]{1,0:T(8,128)}, f32[256,256]{1,0:T(8,128)S(1)}, u32[]{:S(2)}) copy-start(f32[256,256]{1,0:T(8,128)S(1)} %broadcast_multiply_fusion.4) | copy-start | bytes 786436
  121.7 38.1 %all-to-all-start.1 = ((f32[16,16,1280]{2,1,0:T(8,128)}), f32[16,16,1280]{2,1,0:T(8,128)}, u32[]{:S(2)}, u32[]{:S(2)}) async-start(f32[16,16,1280]{2,1,0:T(8,128)} %broadcast_in_dim.32), calls=%async_computation.1 | async-start | bytes 2621440 | tf_op jit(solution)/shard_map/all_to_all | solution.py:19
  128.1 140.4 %all-gather.15.cloned.1.call-start = ((), (), s32[]{:S(2)}) async-start(), calls=%async_computation.7 | async-start | bytes 4456448 | tf_op jit(solution)/shard_map/all_gather | solution.py:27
  130.9 1.7 copy-start.11
  130.9 1.7 copy-start.28
  169.9 46.4 %copy-start.14 = (f32[256,256]{1,0:T(8,128)}, f32[256,256]{1,0:T(8,128)S(1)}, u32[]{:S(2)}) copy-start(f32[256,256]{1,0:T(8,128)S(1)} %reduce_sum.280) | copy-start | bytes 786436
  216.3 3.9 copy-start.22
  220.2 55.6 %copy-start.1 = (f32[16,16,1280]{2,1,0:T(8,128)}, f32[16,16,1280]{2,1,0:T(8,128)S(1)}, u32[]{:S(2)}) copy-start(f32[16,16,1280]{2,1,0:T(8,128)S(1)} %get-tuple-element.15) | copy-start | bytes 3932164
  223.9 38.3 %all-to-all-start.2 = ((f32[16,16,1280]{2,1,0:T(8,128)}), f32[16,16,1280]{2,1,0:T(8,128)}, u32[]{:S(2)}, u32[]{:S(2)}) async-start(f32[16,16,1280]{2,1,0:T(8,128)} %broadcast_in_dim.33), calls=%async_computation.2 | async-start | bytes 2621440 | tf_op jit(solution)/shard_map/all_to_all | solution.py:19
  230.5 150.5 %all-gather.17.cloned.1.call-start = ((), (), s32[]{:S(2)}) async-start(), calls=%async_computation.8 | async-start | bytes 4456448 | tf_op jit(solution)/shard_map/all_gather | solution.py:27
  235.2 1.7 copy-start.7
  235.2 1.8 copy-start.12
  235.2 1.8 copy-start.29
  326.6 5.3 copy-start.23
  331.9 1.7 copy-start.17
  334.8 38.5 %all-to-all-start.3 = ((f32[16,16,1280]{2,1,0:T(8,128)}), f32[16,16,1280]{2,1,0:T(8,128)}, u32[]{:S(2)}, u32[]{:S(2)}) async-start(f32[16,16,1280]{2,1,0:T(8,128)} %broadcast_in_dim.34), calls=%async_computation.3 | async-start | bytes 2621440 | tf_op jit(solution)/shard_map/all_to_all | solution.py:19
  341.5 147.8 %all-gather.19.cloned.1.call-start = ((), (), s32[]{:S(2)}) async-start(), calls=%async_computation.9 | async-start | bytes 4456448 | tf_op jit(solution)/shard_map/all_gather | solution.py:27
  345.1 1.1 copy-start.8
  345.1 1.1 copy-start.30
  351.5 24.8 %copy-start.2 = (f32[16,16,1280]{2,1,0:T(8,128)S(1)}, f32[16,16,1280]{2,1,0:T(8,128)}, u32[]{:S(2)}) copy-start(f32[16,16,1280]{2,1,0:T(8,128)} %get-tuple-element.12) | copy-start | bytes 3932164
  437.0 4.9 copy-start.24
  440.8 1.1 copy-start.4
  440.8 2.7 copy-start.18
  444.7 6.0 %copy-start.5 = (f32[16,16,1280]{2,1,0:T(8,128)S(1)}, f32[16,16,1280]{2,1,0:T(8,128)}, u32[]{:S(2)}) copy-start(f32[16,16,1280]{2,1,0:T(8,128)} %copy-done.4) | copy-start | bytes 3932164
  444.7 37.7 %all-to-all-start.4 = ((f32[16,16,1280]{2,1,0:T(8,128)}), f32[16,16,1280]{2,1,0:T(8,128)}, u32[]{:S(2)}, u32[]{:S(2)}) async-start(f32[16,16,1280]{2,1,0:T(8,128)} %broadcast_in_dim.35), calls=%async_computation.4 | async-start | bytes 2621440 | tf_op jit(solution)/shard_map/all_to_all | solution.py:19
  454.0 1.1 copy-start.9
  454.1 1.1 copy-start.31
  492.5 4.3 copy-start.3
Sparse Core Ops, SparseCore 0:
  10.4 54.4 all-gather.10
  120.7 46.2 all-gather.12
  222.0 46.4 all-gather.14
  333.7 46.8 all-gather.16
  443.7 45.6 all-gather.18
where the time goes:
time: 573 us; the launch traced here: 564 us
  blocking collectives  211 us (37%)
  waiting for transfers between devices  125 us (22%)
  other arithmetic  71.2 us (12%)
  local copies, waits for them, and re-layouts  47.5 us (8%)
  starting transfers between devices  38.5 us (7%)
  matrix products  36.9 us (6%)
  between operations  33.8 us (6%)
    psum x25, blocking collectives, by_axis(): value = lax.psum(value, axis)  211 us
    all_to_all x5, waiting for transfers between devices, copy_for_each(): return lax.all_to_all(copies, axis, split_axis=0, concat_axis=0, tiled=True)  111 us
    all_to_all x5, starting transfers between devices, copy_for_each(): return lax.all_to_all(copies, axis, split_axis=0, concat_axis=0, tiled=True)  37.3 us
    dot_general x5, matrix products, local(): jnp.dot(prices.reshape(row_count, zone_count), onehot.T, precision=lax.Pr...  22.2 us
    reduce_sum x5, other arithmetic, local(): gap_local = jnp.sum(dispatch * low_dual + (capacity - dispatch) * high_dual)  16.9 us
    reduce_sum x5, other arithmetic, over_pieces(): return blocks.sum(axis=0)  14.5 us
    all_gather x5, waiting for transfers between devices, over_pieces(): blocks = lax.all_gather(value, axis)  13.8 us
    reshape x5, local copies, waits for them, and re-layouts, local(): (own_part + cross_part * block_mask[None, :, None]).reshape(local_scen, p...  12.1 us
  transfers between devices with their start and end apart: 10, of which 8 were waited for; matrix products, arithmetic and copies ran while one was open for 13% of the time, Pallas kernels for 0%

commit v1 on v0

--- a/solution.py
+++ b/solution.py
@@ -30,7 +30,7 @@
 
 def by_axis(value, axes):
     for axis in axes:
-        value = lax.psum(value, axis)
+        value = jnp.sum(lax.all_gather(value, axis), axis=0)
     return value
 
 

time: 573 us -> 620 us (1.082)
  local copies, waits for them, and re-layouts: 47.5 us -> 82.3 us
  other arithmetic: 71.2 us -> 85.3 us
  waiting for transfers between devices: 125 us -> 118 us
    psum x25 -> x0, blocking collectives: 211 us -> none  [by_axis(): value = lax.psum(value, axis)]
    unnamed x0 -> x25, blocking collectives: none -> 211 us
    unnamed x70 -> x130, local copies, waits for them, and re-layouts: 3.36 us -> 24.4 us
    all_gather x0 -> x25, local copies, waits for them, and re-layouts: none -> 13.9 us  [by_axis(): value = jnp.sum(lax.all_gather(value, axis), axis=0)]
    reduce_sum x0 -> x25, other arithmetic: none -> 12.4 us  [by_axis(): value = jnp.sum(lax.all_gather(value, axis), axis=0)]
    unnamed x0 -> x5, other arithmetic: none -> 9.17 us
    another operation x5 -> x0, other arithmetic: 7.5 us -> none  [local(): stacked = jnp.stack([gap_local, dual_local, primal_local])]
    all_to_all x5, waiting for transfers between devices: 111 us -> 104 us  [copy_for_each(): return lax.all_to_all(copies, axis, split_axis=0, concat_axis=0, tiled=True)]
where the time goes in v1:
time: 620 us; the launch traced here: 609 us
  blocking collectives  211 us (34%)
  waiting for transfers between devices  118 us (19%)
  other arithmetic  85.3 us (14%)
  local copies, waits for them, and re-layouts  82.3 us (13%)
  starting transfers between devices  38.5 us (6%)
  between operations  37.3 us (6%)
  matrix products  36.9 us (6%)
    unnamed x25, blocking collectives  211 us
    all_to_all x5, waiting for transfers between devices, copy_for_each(): return lax.all_to_all(copies, axis, split_axis=0, concat_axis=0, tiled=True)  104 us
    all_to_all x5, starting transfers between devices, copy_for_each(): return lax.all_to_all(copies, axis, split_axis=0, concat_axis=0, tiled=True)  37.6 us
    unnamed x130, local copies, waits for them, and re-layouts  24.4 us
    dot_general x5, matrix products, local(): jnp.dot(prices.reshape(row_count, zone_count), onehot.T, precision=lax.Pr...  22.2 us
    reduce_sum x5, other arithmetic, local(): gap_local = jnp.sum(dispatch * low_dual + (capacity - dispatch) * high_dual)  16.9 us
    reduce_sum x5, other arithmetic, over_pieces(): return blocks.sum(axis=0)  14.5 us
    all_gather x25, local copies, waits for them, and re-layouts, by_axis(): value = jnp.sum(lax.all_gather(value, axis), axis=0)  13.9 us
  transfers between devices with their start and end apart: 10, of which 8 were waited for; matrix products, arithmetic and copies ran while one was open for 13% of the time, Pallas kernels for 0%

profile of v1, /device:TPU:1, one launch (start us, length us, event | category | flops | bytes accessed | tf_op | source)
XLA Modules:
  0.0 609.3 jit_solution(71296454570223554)
XLA Ops:
  11.2 11.8 %all-to-all-start = ((f32[16,16,1280]{2,1,0:T(8,128)}), f32[16,16,1280]{2,1,0:T(8,128)}, u32[]{:S(2)}, u32[]{:S(2)}) async-start(f32[16,16,1280]{2,1,0:T(8,128)} %broadcast_in_dim.30), calls=%async_computation | async-start | bytes 2621440 | tf_op jit(solution)/shard_map/all_to_all | solution.py:19
  25.3 2.1 copy.38
  37.4 17.2 %all-to-all-done = f32[16,16,1280]{2,1,0:T(8,128)} async-done(((f32[16,16,1280]{2,1,0:T(8,128)}), f32[16,16,1280]{2,1,0:T(8,128)}, u32[]{:S(2)}, u32[]{:S(2)}) %all-to-all-start) | async-done | bytes 1310752 | tf_op jit(solution)/shard_map/all_to_all | solution.py:19
  56.0 2.6 multiply_reduce_fusion.4
  58.7 6.2 %all-gather.36.cloned.1.call-done = f32[4096,256]{1,0:T(8,128)} async-done(((f32[256,256]{1,0:T(8,128)}), f32[4096,256]{1,0:T(8,128)}) %all-gather.36.cloned.1.call-update) | async-done | bytes 4194320 | tf_op jit(solution)/shard_map/all_gather | solution.py:27
  64.9 2.5 reduce_sum.499
  70.1 14.7 %all-reduce = f32[24]{0:T(128)S(1)} all-reduce(f32[24]{0:T(128)S(1)} %maximum_dynamic-update-slice_fusion), channel_id=3, replica_groups=mesh['scen_0'=8,'scen_1'=2,'gen_0'=2,'gen_1'=4,'gen_2'=2] {'scen_0'}, use_global_device_ids=true, to_apply=%add | all-reduce | flops 24 | bytes 192
  85.8 5.3 all-reduce.1
  92.0 3.9 all-reduce.2
  96.9 6.9 %all-reduce.3 = f32[12]{0:T(128)S(1)} all-reduce(f32[12]{0:T(128)S(1)} %dynamic-update-slice.3), channel_id=6, replica_groups=mesh['scen_0'=8,'scen_1'=2,'gen_0'=2,'gen_1'=4,'gen_2'=2] {'gen_1'}, use_global_device_ids=true, to_apply=%add.3 | all-reduce | flops 12 | bytes 96
  104.3 10.4 %all-reduce.4 = f32[6]{0:T(128)S(1)} all-reduce(f32[6]{0:T(128)S(1)} %dynamic-update-slice.4), channel_id=7, replica_groups=mesh['scen_0'=8,'scen_1'=2,'gen_0'=2,'gen_1'=4,'gen_2'=2] {'gen_2'}, use_global_device_ids=true, to_apply=%add.4 | all-reduce | flops 6 | bytes 48
  116.6 2.9 add_reduce_fusion.3
  122.4 6.5 %all-to-all-start.1 = ((f32[16,16,1280]{2,1,0:T(8,128)}), f32[16,16,1280]{2,1,0:T(8,128)}, u32[]{:S(2)}, u32[]{:S(2)}) async-start(f32[16,16,1280]{2,1,0:T(8,128)} %broadcast_in_dim.32), calls=%async_computation.1 | async-start | bytes 2621440 | tf_op jit(solution)/shard_map/all_to_all | solution.py:19
  133.7 2.1 copy.41
  137.7 23.0 %all-to-all-done.1 = f32[16,16,1280]{2,1,0:T(8,128)} async-done(((f32[16,16,1280]{2,1,0:T(8,128)}), f32[16,16,1280]{2,1,0:T(8,128)}, u32[]{:S(2)}, u32[]{:S(2)}) %all-to-all-start.1) | async-done | bytes 1310752 | tf_op jit(solution)/shard_map/all_to_all | solution.py:19
  163.7 4.5 multiply_reduce_fusion.3
  168.2 2.5 reduce_sum.510
  173.4 14.5 %all-reduce.5 = f32[24]{0:T(128)S(1)} all-reduce(f32[24]{0:T(128)S(1)} %maximum_dynamic-update-slice_fusion.1), channel_id=9, replica_groups=mesh['scen_0'=8,'scen_1'=2,'gen_0'=2,'gen_1'=4,'gen_2'=2] {'scen_0'}, use_global_device_ids=true, to_apply=%add.5 | all-reduce | flops 24 | bytes 192
  188.2 5.3 all-reduce.6
  194.5 4.1 all-reduce.7
  199.6 6.3 %all-reduce.8 = f32[12]{0:T(128)S(1)} all-reduce(f32[12]{0:T(128)S(1)} %dynamic-update-slice.8), channel_id=12, replica_groups=mesh['scen_0'=8,'scen_1'=2,'gen_0'=2,'gen_1'=4,'gen_2'=2] {'gen_1'}, use_global_device_ids=true, to_apply=%add.8 | all-reduce | flops 12 | bytes 96
  206.3 10.2 %all-reduce.9 = f32[6]{0:T(128)S(1)} all-reduce(f32[6]{0:T(128)S(1)} %dynamic-update-slice.9), channel_id=13, replica_groups=mesh['scen_0'=8,'scen_1'=2,'gen_0'=2,'gen_1'=4,'gen_2'=2] {'gen_2'}, use_global_device_ids=true, to_apply=%add.9 | all-reduce | flops 6 | bytes 48
  218.5 3.9 add_reduce_fusion.2
  226.2 6.6 %all-to-all-start.2 = ((f32[16,16,1280]{2,1,0:T(8,128)}), f32[16,16,1280]{2,1,0:T(8,128)}, u32[]{:S(2)}, u32[]{:S(2)}) async-start(f32[16,16,1280]{2,1,0:T(8,128)} %broadcast_in_dim.33), calls=%async_computation.2 | async-start | bytes 2621440 | tf_op jit(solution)/shard_map/all_to_all | solution.py:19
  234.6 2.5 reshape.274
  239.3 2.1 copy.44
  241.4 2.7 reshape.275
  244.2 20.4 %all-to-all-done.2 = f32[16,16,1280]{2,1,0:T(8,128)} async-done(((f32[16,16,1280]{2,1,0:T(8,128)}), f32[16,16,1280]{2,1,0:T(8,128)}, u32[]{:S(2)}, u32[]{:S(2)}) %all-to-all-start.2) | async-done | bytes 1310752 | tf_op jit(solution)/shard_map/all_to_all | solution.py:19
  268.2 2.8 all-gather.40.cloned.1.call-done
  271.0 3.2 reduce_sum.521
  275.2 2.5 divide_add_fusion.3
  278.3 5.3 multiply_reduce_fusion.2
  285.0 14.6 %all-reduce.10 = f32[24]{0:T(128)S(1)} all-reduce(f32[24]{0:T(128)S(1)} %maximum_dynamic-update-slice_fusion.2), channel_id=15, replica_groups=mesh['scen_0'=8,'scen_1'=2,'gen_0'=2,'gen_1'=4,'gen_2'=2] {'scen_0'}, use_global_device_ids=true, to_apply=%add.10 | all-reduce | flops 24 | bytes 192
  300.0 5.3 all-reduce.11
  306.3 3.8 all-reduce.12
  311.1 6.6 %all-reduce.13 = f32[12]{0:T(128)S(1)} all-reduce(f32[12]{0:T(128)S(1)} %dynamic-update-slice.13), channel_id=18, replica_groups=mesh['scen_0'=8,'scen_1'=2,'gen_0'=2,'gen_1'=4,'gen_2'=2] {'gen_1'}, use_global_device_ids=true, to_apply=%add.13 | all-reduce | flops 12 | bytes 96
  318.1 10.5 %all-reduce.14 = f32[6]{0:T(128)S(1)} all-reduce(f32[6]{0:T(128)S(1)} %dynamic-update-slice.14), channel_id=19, replica_groups=mesh['scen_0'=8,'scen_1'=2,'gen_0'=2,'gen_1'=4,'gen_2'=2] {'gen_2'}, use_global_device_ids=true, to_apply=%add.14 | all-reduce | flops 6 | bytes 48
  330.7 5.3 add_reduce_fusion.1
  339.0 6.7 %all-to-all-start.3 = ((f32[16,16,1280]{2,1,0:T(8,128)}), f32[16,16,1280]{2,1,0:T(8,128)}, u32[]{:S(2)}, u32[]{:S(2)}) async-start(f32[16,16,1280]{2,1,0:T(8,128)} %broadcast_in_dim.34), calls=%async_computation.3 | async-start | bytes 2621440 | tf_op jit(solution)/shard_map/all_to_all | solution.py:19
  353.0 2.7 reshape.278
  355.7 21.7 %all-to-all-done.3 = f32[16,16,1280]{2,1,0:T(8,128)} async-done(((f32[16,16,1280]{2,1,0:T(8,128)}), f32[16,16,1280]{2,1,0:T(8,128)}, u32[]{:S(2)}, u32[]{:S(2)}) %all-to-all-start.3) | async-done | bytes 1310752 | tf_op jit(solution)/shard_map/all_to_all | solution.py:19
  380.4 4.8 multiply_reduce_fusion.1
  385.1 3.2 reduce_sum.532
  391.1 2.6 maximum_dynamic-update-slice_fusion.3
  393.7 15.2 %all-reduce.15 = f32[24]{0:T(128)} all-reduce(f32[24]{0:T(128)} %maximum_dynamic-update-slice_fusion.3), channel_id=21, replica_groups=mesh['scen_0'=8,'scen_1'=2,'gen_0'=2,'gen_1'=4,'gen_2'=2] {'scen_0'}, use_global_device_ids=true, to_apply=%add.15 | all-reduce | flops 24 | bytes 192
  413.2 5.9 all-reduce.16
  424.0 4.5 all-reduce.17
  433.5 7.2 %all-reduce.18 = f32[12]{0:T(128)} all-reduce(f32[12]{0:T(128)} %dynamic-update-slice.18), channel_id=24, replica_groups=mesh['scen_0'=8,'scen_1'=2,'gen_0'=2,'gen_1'=4,'gen_2'=2] {'gen_1'}, use_global_device_ids=true, to_apply=%add.18 | all-reduce | flops 12 | bytes 96
  445.0 11.9 %all-reduce.19 = f32[6]{0:T(128)} all-reduce(f32[6]{0:T(128)} %dynamic-update-slice.19), channel_id=25, replica_groups=mesh['scen_0'=8,'scen_1'=2,'gen_0'=2,'gen_1'=4,'gen_2'=2] {'gen_2'}, use_global_device_ids=true, to_apply=%add.19 | all-reduce | flops 6 | bytes 48
  462.0 3.8 add_reduce_fusion
  469.8 6.1 all-to-all-start.4
  482.8 2.8 reshape.281
  485.6 22.0 %all-to-all-done.4 = f32[16,16,1280]{2,1,0:T(8,128)} async-done(((f32[16,16,1280]{2,1,0:T(8,128)}), f32[16,16,1280]{2,1,0:T(8,128)}, u32[]{:S(2)}, u32[]{:S(2)}) %all-to-all-start.4) | async-done | bytes 1310752 | tf_op jit(solution)/shard_map/all_to_all | solution.py:19
  509.6 4.8 all-gather.44.cloned.1.call-done
  514.4 3.2 reduce_sum.543
  518.6 2.6 multiply_reduce_fusion.5
  522.0 5.0 multiply_reduce_fusion
  527.4 2.4 maximum_dynamic-update-slice_fusion.4
  529.8 15.2 %all-reduce.20 = f32[24]{0:T(128)} all-reduce(f32[24]{0:T(128)} %maximum_dynamic-update-slice_fusion.4), channel_id=27, replica_groups=mesh['scen_0'=8,'scen_1'=2,'gen_0'=2,'gen_1'=4,'gen_2'=2] {'scen_0'}, use_global_device_ids=true, to_apply=%add.20 | all-reduce | flops 24 | bytes 192
  549.4 5.9 all-reduce.21
  560.0 4.4 all-reduce.22
  569.3 7.4 %all-reduce.23 = f32[12]{0:T(128)} all-reduce(f32[12]{0:T(128)} %dynamic-update-slice.23), channel_id=30, replica_groups=mesh['scen_0'=8,'scen_1'=2,'gen_0'=2,'gen_1'=4,'gen_2'=2] {'gen_1'}, use_global_device_ids=true, to_apply=%add.23 | all-reduce | flops 12 | bytes 96
  580.9 10.8 %all-reduce.24 = f32[6]{0:T(128)} all-reduce(f32[6]{0:T(128)} %dynamic-update-slice.24), channel_id=31, replica_groups=mesh['scen_0'=8,'scen_1'=2,'gen_0'=2,'gen_1'=4,'gen_2'=2] {'gen_2'}, use_global_device_ids=true, to_apply=%add.24 | all-reduce | flops 6 | bytes 48
  598.5 3.7 maximum_minimum_fusion
  (262 shorter events, 121.7 us)
Async XLA Ops:
  7.2 16.7 %copy-start = (bf16[5,256,256]{2,1,0:T(8,128)(2,1)S(1)}, bf16[5,256,256]{2,1,0:T(8,128)(2,1)}, u32[]{:S(2)}) copy-start(bf16[5,256,256]{2,1,0:T(8,128)(2,1)} %param.14) | copy-start | bytes 1966084
  7.2 1.0 copy-start.21
  7.2 57.7 %all-gather.36.cloned.1.call-start = ((), (), s32[]{:S(2)}) async-start(), calls=%async_computation.5 | async-start | bytes 4456448 | tf_op jit(solution)/shard_map/all_gather | solution.py:27
  8.1 1.8 copy-start.16
  11.2 43.4 %all-to-all-start = ((f32[16,16,1280]{2,1,0:T(8,128)}), f32[16,16,1280]{2,1,0:T(8,128)}, u32[]{:S(2)}, u32[]{:S(2)}) async-start(f32[16,16,1280]{2,1,0:T(8,128)} %broadcast_in_dim.30), calls=%async_computation | async-start | bytes 2621440 | tf_op jit(solution)/shard_map/all_to_all | solution.py:19
  23.0 0.8 copy-start.34
  23.0 145.2 %all-gather.38.cloned.1.call-start = ((), (), s32[]{:S(2)}) async-start(), calls=%async_computation.6 | async-start | bytes 4456448 | tf_op jit(solution)/shard_map/all_gather | solution.py:27
  23.9 1.5 copy-start.27
  23.9 1.1 copy-start.6
  27.5 2.0 copy-start.39
  27.5 2.6 copy-start.38
  27.5 4.5 copy-start.37
  27.5 5.8 copy-start.36
  27.5 7.0 %copy-start.35 = (u32[256]{0:T(256)S(1)}, u32[256]{0:T(256)}, u32[]{:S(2)}) copy-start(u32[256]{0:T(256)} %constant.146) | copy-start | bytes 3076
  27.5 7.6 %copy-start.32 = (s32[5]{0:T(128)S(1)}, s32[5]{0:T(128)}, u32[]{:S(2)}) copy-start(s32[5]{0:T(128)} %param.18) | copy-start | bytes 64
  27.5 8.3 %copy-start.33 = (s32[5]{0:T(128)S(1)}, s32[5]{0:T(128)}, u32[]{:S(2)}) copy-start(s32[5]{0:T(128)} %param.19) | copy-start | bytes 64
  27.5 9.9 %copy-start.26 = (f32[1280]{0:T(1024)S(1)}, f32[1280]{0:T(1024)}, u32[]{:S(2)}) copy-start(f32[1280]{0:T(1024)} %param.12) | copy-start | bytes 15364
  29.5 26.5 %copy-start.25 = (f32[16,1280]{1,0:T(8,128)S(1)}, f32[16,1280]{1,0:T(8,128)}, u32[]{:S(2)}) copy-start(f32[16,1280]{1,0:T(8,128)} %param.11) | copy-start | bytes 245764
  37.4 79.2 %copy-start.19 = (f32[1280]{0:T(1024)}, f32[1280]{0:T(1024)S(1)}, u32[]{:S(2)}) copy-start(f32[1280]{0:T(1024)S(1)} %get-tuple-element.24) | copy-start | bytes 15364
  37.4 79.2 %copy-start.20 = (f32[1280]{0:T(1024)}, f32[1280]{0:T(1024)S(1)}, u32[]{:S(2)}) copy-start(f32[1280]{0:T(1024)S(1)} %get-tuple-element.25) | copy-start | bytes 15364
  64.9 2.6 copy-start.10
  67.4 49.2 %copy-start.13 = (f32[256,256]{1,0:T(8,128)}, f32[256,256]{1,0:T(8,128)S(1)}, u32[]{:S(2)}) copy-start(f32[256,256]{1,0:T(8,128)S(1)} %reduce_sum.499) | copy-start | bytes 786436
  67.4 49.2 %copy-start.15 = (f32[256,256]{1,0:T(8,128)}, f32[256,256]{1,0:T(8,128)S(1)}, u32[]{:S(2)}) copy-start(f32[256,256]{1,0:T(8,128)S(1)} %broadcast_multiply_fusion.4) | copy-start | bytes 786436
  122.4 38.3 %all-to-all-start.1 = ((f32[16,16,1280]{2,1,0:T(8,128)}), f32[16,16,1280]{2,1,0:T(8,128)}, u32[]{:S(2)}, u32[]{:S(2)}) async-start(f32[16,16,1280]{2,1,0:T(8,128)} %broadcast_in_dim.32), calls=%async_computation.1 | async-start | bytes 2621440 | tf_op jit(solution)/shard_map/all_to_all | solution.py:19
  129.0 142.1 %all-gather.40.cloned.1.call-start = ((), (), s32[]{:S(2)}) async-start(), calls=%async_computation.7 | async-start | bytes 4456448 | tf_op jit(solution)/shard_map/all_gather | solution.py:27
  131.6 1.7 copy-start.11
  131.6 1.7 copy-start.28
  170.7 47.9 %copy-start.14 = (f32[256,256]{1,0:T(8,128)}, f32[256,256]{1,0:T(8,128)S(1)}, u32[]{:S(2)}) copy-start(f32[256,256]{1,0:T(8,128)S(1)} %reduce_sum.510) | copy-start | bytes 786436
  218.5 3.9 copy-start.22
  222.4 55.9 %copy-start.1 = (f32[16,16,1280]{2,1,0:T(8,128)}, f32[16,16,1280]{2,1,0:T(8,128)S(1)}, u32[]{:S(2)}) copy-start(f32[16,16,1280]{2,1,0:T(8,128)S(1)} %get-tuple-element.15) | copy-start | bytes 3932164
  226.2 38.4 %all-to-all-start.2 = ((f32[16,16,1280]{2,1,0:T(8,128)}), f32[16,16,1280]{2,1,0:T(8,128)}, u32[]{:S(2)}, u32[]{:S(2)}) async-start(f32[16,16,1280]{2,1,0:T(8,128)} %broadcast_in_dim.33), calls=%async_computation.2 | async-start | bytes 2621440 | tf_op jit(solution)/shard_map/all_to_all | solution.py:19
  232.8 152.3 %all-gather.42.cloned.1.call-start = ((), (), s32[]{:S(2)}) async-start(), calls=%async_computation.8 | async-start | bytes 4456448 | tf_op jit(solution)/shard_map/all_gather | solution.py:27
  237.1 1.8 copy-start.7
  237.1 1.8 copy-start.12
  237.1 1.8 copy-start.29
  330.7 5.3 copy-start.23
  336.0 1.7 copy-start.17
  339.0 38.5 %all-to-all-start.3 = ((f32[16,16,1280]{2,1,0:T(8,128)}), f32[16,16,1280]{2,1,0:T(8,128)}, u32[]{:S(2)}, u32[]{:S(2)}) async-start(f32[16,16,1280]{2,1,0:T(8,128)} %broadcast_in_dim.34), calls=%async_computation.3 | async-start | bytes 2621440 | tf_op jit(solution)/shard_map/all_to_all | solution.py:19
  345.6 168.8 %all-gather.44.cloned.1.call-start = ((), (), s32[]{:S(2)}) async-start(), calls=%async_computation.9 | async-start | bytes 4456448 | tf_op jit(solution)/shard_map/all_gather | solution.py:27
  349.4 1.1 copy-start.8
  349.4 1.1 copy-start.30
  355.7 24.6 %copy-start.2 = (f32[16,16,1280]{2,1,0:T(8,128)S(1)}, f32[16,16,1280]{2,1,0:T(8,128)}, u32[]{:S(2)}) copy-start(f32[16,16,1280]{2,1,0:T(8,128)} %get-tuple-element.12) | copy-start | bytes 3932164
  462.0 4.9 copy-start.24
  465.8 1.1 copy-start.4
  465.8 2.7 copy-start.18
  469.8 6.1 copy-start.5
  469.8 37.8 %all-to-all-start.4 = ((f32[16,16,1280]{2,1,0:T(8,128)}), f32[16,16,1280]{2,1,0:T(8,128)}, u32[]{:S(2)}, u32[]{:S(2)}) async-start(f32[16,16,1280]{2,1,0:T(8,128)} %broadcast_in_dim.35), calls=%async_computation.4 | async-start | bytes 2621440 | tf_op jit(solution)/shard_map/all_to_all | solution.py:19
  479.1 1.1 copy-start.9
  479.2 1.1 copy-start.31
  517.6 4.4 copy-start.3
Sparse Core Ops, SparseCore 0:
  10.4 54.4 all-gather.35
  121.4 46.3 all-gather.37
  224.2 46.7 all-gather.39
  337.9 46.8 all-gather.41
  468.7 45.6 all-gather.43
